TPU v7x, 32 devices: a whole 2x2x4 slice. The times are simulated.
32 devices in a mesh: groups: 2 (over x), blk: 16 (over z, y, core).
Axes of the slice: x: 2, y: 2, z: 4, core: 2. Of those that a mesh axis runs over, the one named last changes fastest.
Arguments:
- queries: bfloat16 [1024, 8192], P('groups', 'blk'), parts along dimension 0, may hold values from -41 to 41
- prefix_kv: bfloat16 [32, 64, 8, 256], P(('groups', 'blk')), parts along dimension 0, may hold values from -6 to 6
- page_counts: int32 [8], P('groups'), parts along dimension 0, may hold values from 1 to 8, 16 in all
- request_prefix: int32 [1024, 1], P(('groups', 'blk')), parts along dimension 0, may hold values from 0 to 3
- suffix_kv: bfloat16 [1024, 64, 8, 256], P(('groups', 'blk')), parts along dimension 0, may hold values from -6 to 6
- suffix_len: int32 [1024], P(('groups', 'blk')), parts along dimension 0, may hold values from 2 to 64, as said below
Outputs:
- attended: bfloat16 [1024, 8192], P('groups', 'blk'), parts along dimension 0
There are 2 independent parts, one for each index of `groups`. A program takes and returns all parts, laid end to end along the dimension named above; each array names one. Nothing has to cross between parts.
Inputs may be any that keep to these rules, and one draw needn't show every extreme that they name: `page_counts`: the counts sum to 16; the largest is exactly half of 16. `request_prefix`: every prefix is named by some request. `suffix_len`: the requests of one device (aligned blocks of 32) include one with 64 live positions.
All inputs are finite; a program needn't handle non-finite values.
Results may differ from a plain program's by a relative error of at most 0.013.
Values may be sent and summed in bfloat16 or wider, within the bound.
A program may use at most 64 MiB of HBM per device.

v0:
```python
import functools
import math

import jax
import jax.numpy as jnp
from jax import lax
from jax.experimental import pallas as pl
from jax.experimental.pallas import tpu as pltpu
from jax.sharding import PartitionSpec as P

neg_large = -1e30


def div(x, k):
    return jnp.right_shift(x, k.bit_length() - 1) if k & (k - 1) == 0 else x // k


def mod(x, k):
    return jnp.bitwise_and(x, k - 1) if k & (k - 1) == 0 else lax.rem(x, k)


MESH = pl.DeviceIdType.MESH
CHUNKS = 2
LANES = 128


def kernel(
    n, q_ref, kv_ref, rp_ref, pc_ref, suf_ref, len_ref, out_ref,
    home, order, back, qrecv, qperm, operm, retsrc, retrecv, pool, suf, own_recv, own_col,
    stats, stats_src, stats_recv, mix, top, total,
    q_send, q_recv_sem, own_send, own_recv_sem, kv_send, kv_recv, fw_send,
    ret_send, ret_recv, st_send, st_recv, suf_sem,
):
    me = lax.axis_index("blk")
    partner = me + 1 - 2 * lax.rem(me, 2)
    parity = lax.rem(me, 2)
    rows_all, width = q_ref.shape
    req_dev = rows_all // n
    part = req_dev // CHUNKS
    kv_heads, page_len, kv_width = home.shape
    head_dim = kv_width // 2
    per_dev = width // head_dim
    heads = per_dev * n
    group_size = heads // kv_heads
    share = n // kv_heads
    half = share // 2
    cols = suf_ref.shape[1]
    scale = head_dim ** -0.5

    def suf_copy(r):
        return pltpu.make_async_copy(suf_ref.at[r], suf.at[r], suf_sem.at[r])

    @pl.loop(0, req_dev)
    def _(r):
        suf_copy(r).start()

    def iota(shape, dim):
        return lax.broadcasted_iota(jnp.int32, shape, dim)

    barrier = pltpu.get_barrier_semaphore()

    @pl.loop(1, n)
    def _(k):
        pl.semaphore_signal(
            barrier, inc=1, device_id={"blk": lax.rem(me + k, n)}, device_id_type=MESH
        )

    pl.semaphore_wait(barrier, n - 1)

    def send(src, dst, s_sem, r_sem, peer):
        return pltpu.make_async_remote_copy(
            src_ref=src, dst_ref=dst, send_sem=s_sem, recv_sem=r_sem,
            device_id={"blk": peer}, device_id_type=MESH,
        )

    def peer_of(j):
        k = n // 2 + ((j + 1) // 2) * (1 - 2 * lax.rem(j, 2))
        return lax.rem(me + k, n)

    def source_of(j):
        k = n // 2 + ((j + 1) // 2) * (1 - 2 * lax.rem(j, 2))
        return lax.rem(me + n - k, n)

    def q_copy(c, slot, peer):
        rows = pl.ds(pl.multiple_of(peer * req_dev + c * part, part), part)
        return send(
            q_ref.at[rows], qrecv.at[c, slot], q_send.at[c, peer], q_recv_sem.at[c, slot], peer
        )

    def own_copy(slot, peer):
        return send(rp_ref, own_recv.at[slot], own_send.at[peer], own_recv_sem.at[slot], peer)

    def kv_copy(slot, peer):
        return send(
            home.at[peer // share], pool.at[slot], kv_send.at[peer], kv_recv.at[slot], peer
        )

    def fw_copy(slot):
        return send(pool.at[slot], pool.at[slot], fw_send.at[slot], kv_recv.at[slot], partner)

    def fw_own():
        return send(
            home.at[me // share], pool.at[me], fw_send.at[me], kv_recv.at[me], partner
        )

    def ret_copy(c, slot, peer):
        return send(
            retsrc.at[c, peer], retrecv.at[c, slot], ret_send.at[c, peer], ret_recv.at[c, slot],
            peer,
        )

    def st_copy(slot, peer):
        return send(
            stats_src.at[peer], stats_recv.at[slot], st_send.at[peer], st_recv.at[slot], peer
        )

    for c in range(CHUNKS):

        @pl.loop(0, n - 1)
        def _(j, c=c):
            peer = peer_of(j)
            q_copy(c, me, peer).start()
            if c == 0:
                own_copy(me, peer).start()

    for c in range(CHUNKS):
        qrecv[c, me] = q_ref[pl.ds(pl.multiple_of(me * req_dev + c * part, part), part)]
    own_recv[me] = rp_ref[...]

    entries = kv_heads * page_len
    entry, source = iota((entries, entries), 0), iota((entries, entries), 1)
    turn = jnp.where(
        source == mod(entry, page_len) * kv_heads + div(entry, page_len), 1.0, 0.0
    ).astype(jnp.bfloat16)
    turned = jnp.dot(turn, kv_ref[...], preferred_element_type=jnp.float32)
    home[...] = turned.astype(jnp.bfloat16).reshape(home.shape)
    pool[me] = home[me // share]

    @pl.loop(1, n // 2)
    def _(j):
        kv_copy(me, lax.rem(me + 2 * j, n)).start()

    fw_own().start()

    size = part * n
    row_id, col_id = iota((size, size), 0), iota((size, size), 1)
    order[...] = jnp.where(
        col_id == mod(row_id, n) * part + div(row_id, n), 1.0, 0.0
    ).astype(jnp.bfloat16)
    back[...] = jnp.where(
        col_id == mod(row_id, part) * n + div(row_id, part), 1.0, 0.0
    ).astype(jnp.bfloat16)
    stacked = iota((per_dev * n, cols), 0)
    head_of_row = mod(stacked, n) * per_dev + div(stacked, n)
    column = iota((per_dev * n, cols), 1)
    own_kv = div(head_of_row, group_size) == mod(column, kv_heads)
    position = jnp.where(own_kv, div(column, kv_heads), cols)
    lane = iota((n, LANES), 1)
    stats[...] = jnp.zeros_like(stats)

    for c in range(CHUNKS):

        @pl.loop(1, n)
        def _(k, c=c):
            slot = lax.rem(me + k, n)
            q_copy(c, slot, me).wait_recv()

        qperm[...] = jnp.dot(
            order[...], qrecv[c].reshape(size, width), preferred_element_type=jnp.float32
        ).astype(jnp.bfloat16)

        @pl.loop(0, part // 2)
        def _(step, c=c):
            for u in range(2):
                local = step * 2 + u
                r = c * part + local
                suf_copy(r).wait()
                rows = pl.ds(pl.multiple_of(local * n, n), n)
                qr = jnp.concatenate(
                    [qperm[rows, h * head_dim:(h + 1) * head_dim] for h in range(per_dev)], axis=0
                )
                scores = lax.dot_general(
                    qr, suf[r, :, :head_dim], (((1,), (1,)), ((), ())),
                    preferred_element_type=jnp.float32,
                ) * scale
                live = position < len_ref[r]
                scores = jnp.where(live, scores, neg_large)
                top_score = jnp.max(scores, axis=1, keepdims=True)
                weight = jnp.where(live, jnp.exp(scores - top_score), 0.0)
                weight_sum = jnp.sum(weight, axis=1, keepdims=True)
                mixed = jnp.dot(
                    weight.astype(jnp.bfloat16), suf[r, :, head_dim:],
                    preferred_element_type=jnp.float32,
                )
                result = (mixed / weight_sum).astype(jnp.bfloat16)
                level = top_score + jnp.log(weight_sum)
                seen = stats[...]
                for h in range(per_dev):
                    operm[rows, h * head_dim:(h + 1) * head_dim] = result[h * n:(h + 1) * n]
                    seen = jnp.where(
                        lane == h * req_dev + r, level[h * n:(h + 1) * n], seen
                    )
                stats[...] = seen

        returned = jnp.dot(back[...], operm[...], preferred_element_type=jnp.float32)
        retsrc[c] = returned.astype(jnp.bfloat16).reshape(n, part, width)
        if c == CHUNKS - 1:
            for p in range(n):
                stats_src[p] = stats[p:p + 1, :]

        @pl.loop(0, n - 1)
        def _(j, c=c):
            peer = peer_of(j)
            if c == CHUNKS - 1:
                st_copy(me, peer).start()
            ret_copy(c, me, peer).start()

        retrecv[c, me] = retsrc[c, me]
    stats_recv[me] = stats_src[me]

    @pl.loop(1, n // 2)
    def _(j):
        slot = lax.rem(me + 2 * j, n)
        kv_copy(slot, me).wait_recv()
        fw_copy(slot).start()

    @pl.loop(1, n)
    def _(k):
        slot = lax.rem(me + k, n)
        own_copy(slot, me).wait_recv()

    eye = iota((req_dev, req_dev), 0) == iota((req_dev, req_dev), 1)

    @pl.loop(0, n)
    def _(s):
        column_of = jnp.sum(
            jnp.where(eye, own_recv[s].astype(jnp.float32), 0.0), axis=1, keepdims=True
        )
        own_col[pl.ds(pl.multiple_of(s * req_dev, req_dev), req_dev)] = column_of

    @pl.loop(0, n // 2)
    def _(j):
        slot = lax.rem(partner + 2 * j, n)
        fw_copy(slot).wait_recv()

    tokens = n * page_len
    page = div(iota((1, tokens), 1), page_len)
    token_owner = jnp.zeros((1, tokens), jnp.float32)
    end = jnp.int32(0)
    for i in range(pc_ref.shape[0]):
        end = end + pc_ref[i]
        token_owner = token_owner + jnp.where(page >= end, 1.0, 0.0)

    block = max(32, min(rows_all, (256 * 1024) // tokens))

    @pl.loop(0, rows_all // block)
    def _(b):
        rows = pl.ds(pl.multiple_of(b * block, block), block)
        live = own_col[rows] == token_owner
        keys = pool[:, :, :head_dim].reshape(tokens, head_dim)
        values = pool[:, :, head_dim:].reshape(tokens, head_dim)
        for h in range(per_dev):
            scores = lax.dot_general(
                q_ref[rows, h * head_dim:(h + 1) * head_dim], keys, (((1,), (1,)), ((), ())),
                preferred_element_type=jnp.float32,
            ) * scale
            scores = jnp.where(live, scores, neg_large)
            top_score = jnp.max(scores, axis=1, keepdims=True)
            weight = jnp.where(live, jnp.exp(scores - top_score), 0.0)
            top[h, rows] = top_score
            total[h, rows] = jnp.sum(weight, axis=1, keepdims=True)
            mix[rows, h * head_dim:(h + 1) * head_dim] = jnp.dot(
                weight.astype(jnp.bfloat16), values, preferred_element_type=jnp.float32
            )

    sub, lan = iota((req_dev, LANES), 0), iota((req_dev, LANES), 1)

    def gather_in(s):
        rows = pl.ds(pl.multiple_of(s * req_dev, req_dev), req_dev)
        row = stats_recv[s]
        second = retrecv[:, s].reshape(req_dev, width).astype(jnp.float32)
        for h in range(per_dev):
            span = slice(h * head_dim, (h + 1) * head_dim)
            level = jnp.sum(
                jnp.where(lan == h * req_dev + sub, row, 0.0), axis=1, keepdims=True
            )
            top_first = top[h, rows]
            top_score = jnp.maximum(level, top_first)
            factor_second = jnp.exp(level - top_score)
            factor_first = jnp.exp(top_first - top_score)
            inverse = 1.0 / (total[h, rows] * factor_first + factor_second)
            mixed = mix[rows, span] * (factor_first * inverse)
            mixed = mixed + second[:, span] * (factor_second * inverse)
            out_ref[rows, span] = mixed.astype(out_ref.dtype)

    gather_in(me)

    @pl.loop(0, n - 1)
    def _(j):
        slot = source_of(j)
        for c in range(CHUNKS):
            ret_copy(c, slot, me).wait_recv()
        st_copy(slot, me).wait_recv()
        gather_in(slot)

    @pl.loop(1, n)
    def _(k):
        peer = lax.rem(me + k, n)
        for c in range(CHUNKS):
            q_copy(c, me, peer).wait_send()
            ret_copy(c, me, peer).wait_send()
        own_copy(me, peer).wait_send()
        st_copy(me, peer).wait_send()

    @pl.loop(1, n // 2)
    def _(j):
        slot = lax.rem(me + 2 * j, n)
        kv_copy(me, slot).wait_send()
        fw_copy(slot).wait_send()

    fw_own().wait_send()


def body(queries, prefix_kv, page_counts, request_prefix, suffix_kv, suffix_len):
    n = lax.axis_size("blk")
    rows_all, width = queries.shape
    req_dev, suf_len, kv_heads, kv_width = suffix_kv.shape
    head_dim = kv_width // 2
    per_dev = width // head_dim
    page_len = prefix_kv.shape[1]
    part = req_dev // CHUNKS
    page = prefix_kv.reshape(page_len * kv_heads, kv_width)
    cache = suffix_kv.reshape(req_dev, suf_len * kv_heads, kv_width)
    bf16, f32, i32 = jnp.bfloat16, jnp.float32, jnp.int32
    dma = pltpu.SemaphoreType.DMA
    vmem = pl.BlockSpec(memory_space=pltpu.VMEM)
    smem = pl.BlockSpec(memory_space=pltpu.SMEM)
    return pl.pallas_call(
        functools.partial(kernel, n),
        out_shape=jax.ShapeDtypeStruct((rows_all, width), bf16),
        in_specs=[vmem, vmem, vmem, smem, pl.BlockSpec(memory_space=pl.ANY), smem],
        out_specs=vmem,
        scratch_shapes=[
            pltpu.VMEM((kv_heads, page_len, kv_width), bf16),
            pltpu.VMEM((part * n, part * n), bf16),
            pltpu.VMEM((part * n, part * n), bf16),
            pltpu.VMEM((CHUNKS, n, part, width), bf16),
            pltpu.VMEM((part * n, width), bf16),
            pltpu.VMEM((part * n, width), bf16),
            pltpu.VMEM((CHUNKS, n, part, width), bf16),
            pltpu.VMEM((CHUNKS, n, part, width), bf16),
            pltpu.VMEM((n, page_len, kv_width), bf16),
            pltpu.VMEM((req_dev, suf_len * kv_heads, kv_width), bf16),
            pltpu.VMEM((n, 1, req_dev), i32),
            pltpu.VMEM((rows_all, 1), f32),
            pltpu.VMEM((n, LANES), f32),
            pltpu.VMEM((n, 1, LANES), f32),
            pltpu.VMEM((n, 1, LANES), f32),
            pltpu.VMEM((rows_all, width), f32),
            pltpu.VMEM((per_dev, rows_all, 1), f32),
            pltpu.VMEM((per_dev, rows_all, 1), f32),
            dma((CHUNKS, n)), dma((CHUNKS, n)), dma((n,)), dma((n,)), dma((n,)), dma((n,)),
            dma((n,)), dma((CHUNKS, n)), dma((CHUNKS, n)), dma((n,)), dma((n,)), dma((req_dev,)),
        ],
        compiler_params=pltpu.CompilerParams(
            collective_id=0, has_side_effects=True, vmem_limit_bytes=56 * 1024 * 1024
        ),
    )(queries, page, request_prefix.T, page_counts, cache, suffix_len)


def solution(mesh):
    in_specs = (
        P("groups", "blk"),
        P(("groups", "blk"), None, None, None),
        P("groups"),
        P(("groups", "blk"), None),
        P(("groups", "blk"), None, None, None),
        P(("groups", "blk")),
    )
    out_specs = P("groups", "blk")
    return jax.shard_map(body, mesh=mesh, in_specs=in_specs, out_specs=out_specs, check_vma=False)
```

profile of v0, /device:TPU:13, one launch (start us, length us, event | category | flops | bytes accessed | tf_op | source)
XLA Modules:
  0.0 48.3 jit_solution(13563651641117891447)
XLA Ops:
  0.0 46.5 %shard_map.64 = bf16[512,512]{1,0:T(8,128)(2,1)} custom-call(bf16[512,512]{1,0:T(8,128)(2,1)} %q_ref.1, bf16[512,256]{1,0:T(8,128)(2,1)} %bitcast.4, s32[1,32]{1,0:T(1,128)} %bitcast.5, s32[4]{0:T(128)} %pc_ref.1, bf16[32,512,256]{2,1,0:T(8,128)(2,1)} %bitcast.3, s32[32]{0:T(128)} %len_ref.1), custom_call_target="tpu_custom_call" | custom-call | tf_op jit(solution)/shard_map/pallas_call | solution.py:338
  46.5 1.9 %copy.8 = bf16[512,512]{1,0:T(8,128)(2,1)} copy(bf16[512,512]{1,0:T(8,128)(2,1)} %shard_map.64) | data formatting | bytes 1048576
where the time goes:
time: 48.5 us; the launch traced here: 48.3 us
  Pallas kernels  46.5 us (96%)
  local copies, waits for them, and re-layouts  1.87 us (4%)
    pallas_call x1, Pallas kernels, body(): pl.pallas_call(functools.partial(kernel, n), out_shape=jax.ShapeDtypeStru...  46.5 us
    unnamed x1, local copies, waits for them, and re-layouts  1.87 us

commit v1 on v0

v1 whole, which is shorter than its diff:
```python
import functools
import math

import jax
import jax.numpy as jnp
from jax import lax
from jax.experimental import pallas as pl
from jax.experimental.pallas import tpu as pltpu
from jax.sharding import PartitionSpec as P

neg_large = -1e30


def div(x, k):
    return jnp.right_shift(x, k.bit_length() - 1) if k & (k - 1) == 0 else x // k


def mod(x, k):
    return jnp.bitwise_and(x, k - 1) if k & (k - 1) == 0 else lax.rem(x, k)


MESH = pl.DeviceIdType.MESH
CHUNKS = 2
UNROLL = 4
LANES = 128
PREFIX_KI = 256
VMEM_MIB = 56
LOG2E = math.log2(math.e)


def kernel(
    n, q_hbm, kv_hbm, rp_ref, pc_ref, suf_ref, len_ref, out_ref,
    q_ref, kv_ref, home, order, back, qrecv, qperm, operm, retsrc, retrecv, pool, suf, own_recv,
    own_col, stats_src, stats_recv, mix, second_factor, top, total,
    q_send, q_recv_sem, own_send, own_recv_sem, kv_send, kv_recv, fw_send,
    ret_send, ret_recv, st_send, st_recv, suf_sem, in_sem,
):
    me = lax.axis_index("blk")
    partner = me + 1 - 2 * lax.rem(me, 2)
    rows_all, width = q_ref.shape
    req_dev = rows_all // n
    part = req_dev // CHUNKS
    kv_heads, page_len, kv_width = home.shape
    head_dim = kv_width // 2
    per_dev = width // head_dim
    heads = per_dev * n
    group_size = heads // kv_heads
    share = n // kv_heads
    cols = suf_ref.shape[1]
    scale = head_dim ** -0.5 * LOG2E
    power = n & (n - 1) == 0

    def iota(shape, dim):
        return lax.broadcasted_iota(jnp.int32, shape, dim)

    barrier = pltpu.get_barrier_semaphore()

    @pl.loop(1, n)
    def _(k):
        pl.semaphore_signal(
            barrier, inc=1, device_id={"blk": lax.rem(me + k, n)}, device_id_type=MESH
        )

    q_in = pltpu.make_async_copy(q_hbm, q_ref, in_sem.at[0])
    kv_in = pltpu.make_async_copy(kv_hbm, kv_ref, in_sem.at[1])
    q_in.start()
    kv_in.start()

    def suf_copy(r):
        return pltpu.make_async_copy(suf_ref.at[r], suf.at[r], suf_sem.at[r])

    @pl.loop(0, req_dev)
    def _(r):
        suf_copy(r).start()

    def send(src, dst, s_sem, r_sem, peer):
        return pltpu.make_async_remote_copy(
            src_ref=src, dst_ref=dst, send_sem=s_sem, recv_sem=r_sem,
            device_id={"blk": peer}, device_id_type=MESH,
        )

    def peer_of(j):
        return jnp.bitwise_xor(me, j + 1) if power else lax.rem(me + j + 1, n)

    def source_of(j):
        return jnp.bitwise_xor(me, j + 1) if power else lax.rem(me + n - j - 1, n)

    def q_copy(c, slot, peer):
        rows = pl.ds(pl.multiple_of(peer * req_dev + c * part, part), part)
        return send(q_ref.at[rows], qrecv.at[c, slot], q_send.at[c], q_recv_sem.at[c], peer)

    def q_all(c):
        some = qrecv.at[c, pl.ds(0, n - 1)]
        return send(some, some, q_send.at[c], q_recv_sem.at[c], partner)

    def own_copy(slot, peer):
        return send(rp_ref, own_recv.at[slot], own_send, own_recv_sem, peer)

    def own_all():
        some = own_recv.at[pl.ds(0, n - 1)]
        return send(some, some, own_send, own_recv_sem, partner)

    def kv_copy(slot, peer):
        return send(home.at[peer // share], pool.at[slot], kv_send, kv_recv.at[slot], peer)

    def kv_all():
        some = pool.at[pl.ds(0, n // 2 - 1)]
        return send(some, some, kv_send, kv_recv.at[0], partner)

    def fw_copy(slot):
        return send(pool.at[slot], pool.at[slot], fw_send, kv_recv.at[slot], partner)

    def fw_own():
        return send(home.at[me // share], pool.at[me], fw_send, kv_recv.at[me], partner)

    def fw_all():
        some = pool.at[pl.ds(0, n // 2)]
        return send(some, some, fw_send, kv_recv.at[0], partner)

    def ret_copy(c, slot, peer):
        return send(
            retsrc.at[c, peer], retrecv.at[c, slot], ret_send.at[c], ret_recv.at[c, slot], peer
        )

    def ret_all(c):
        some = retsrc.at[c, pl.ds(0, n - 1)]
        return send(some, some, ret_send.at[c], ret_recv.at[c, 0], partner)

    def st_copy(slot, peer):
        return send(stats_src.at[peer], stats_recv.at[slot], st_send, st_recv, peer)

    def st_all():
        some = stats_recv.at[pl.ds(0, n - 1)]
        return send(some, some, st_send, st_recv, partner)

    q_in.wait()
    pl.semaphore_wait(barrier, n - 1)

    for c in range(CHUNKS):

        @pl.loop(0, n - 1)
        def _(j, c=c):
            q_copy(c, me, peer_of(j)).start()

        if c == 0:

            @pl.loop(0, n - 1)
            def _(j):
                own_copy(me, peer_of(j)).start()

    for c in range(CHUNKS):
        qrecv[c, me] = q_ref[pl.ds(pl.multiple_of(me * req_dev + c * part, part), part)]
    own_recv[me] = rp_ref[...]

    kv_in.wait()
    entries = kv_heads * page_len
    entry, source = iota((entries, entries), 0), iota((entries, entries), 1)
    turn = jnp.where(
        source == mod(entry, page_len) * kv_heads + div(entry, page_len), 1.0, 0.0
    ).astype(jnp.bfloat16)
    turned = jnp.dot(turn, kv_ref[...], preferred_element_type=jnp.float32)
    home[...] = turned.astype(jnp.bfloat16).reshape(home.shape)
    pool[me] = home[me // share]

    @pl.loop(1, n // 2)
    def _(j):
        kv_copy(me, lax.rem(me + 2 * j, n)).start()

    fw_own().start()

    size = part * n
    row_id, col_id = iota((size, size), 0), iota((size, size), 1)
    order[...] = jnp.where(
        col_id == mod(row_id, n) * part + div(row_id, n), 1.0, 0.0
    ).astype(jnp.bfloat16)
    back[...] = jnp.where(
        col_id == mod(row_id, part) * n + div(row_id, part), 1.0, 0.0
    ).astype(jnp.bfloat16)
    stacked = iota((per_dev * n, cols), 0)
    head_of_row = mod(stacked, n) * per_dev + div(stacked, n)
    column = iota((per_dev * n, cols), 1)
    own_kv = div(head_of_row, group_size) == mod(column, kv_heads)
    position = jnp.where(own_kv, div(column, kv_heads), cols)
    lane = iota((n, LANES), 1)

    seen = jnp.zeros((n, LANES), jnp.float32)
    for c in range(CHUNKS):
        q_all(c).wait_recv()
        qperm[...] = jnp.dot(
            order[...], qrecv[c].reshape(size, width), preferred_element_type=jnp.float32
        ).astype(jnp.bfloat16)

        def some_requests(step, seen, c=c):
            ids = [step * UNROLL + u for u in range(UNROLL)]
            all_scores = []
            for local in ids:
                r = c * part + local
                suf_copy(r).wait()
                rows = pl.ds(pl.multiple_of(local * n, n), n)
                qr = jnp.concatenate(
                    [qperm[rows, h * head_dim:(h + 1) * head_dim] for h in range(per_dev)], axis=0
                )
                all_scores.append(lax.dot_general(
                    qr, suf[r, :, :head_dim], (((1,), (1,)), ((), ())),
                    preferred_element_type=jnp.float32,
                ))
            for local, scores in zip(ids, all_scores):
                r = c * part + local
                rows = pl.ds(pl.multiple_of(local * n, n), n)
                scores = jnp.where(position < len_ref[r], scores, neg_large)
                top_score = jnp.max(scores, axis=1, keepdims=True)
                weight = jnp.exp2((scores - top_score) * scale)
                weight_sum = jnp.sum(weight, axis=1, keepdims=True)
                mixed = jnp.dot(
                    weight.astype(jnp.bfloat16), suf[r, :, head_dim:],
                    preferred_element_type=jnp.float32,
                )
                result = (mixed * (1.0 / weight_sum)).astype(jnp.bfloat16)
                level = top_score * scale + jnp.log(weight_sum) * LOG2E
                for h in range(per_dev):
                    operm[rows, h * head_dim:(h + 1) * head_dim] = result[h * n:(h + 1) * n]
                    seen = jnp.where(
                        lane == h * req_dev + r, level[h * n:(h + 1) * n], seen
                    )
            return seen

        seen = lax.fori_loop(0, part // UNROLL, some_requests, seen)
        if c == CHUNKS - 1:
            for p in range(n):
                stats_src[p] = seen[p:p + 1, :]

            @pl.loop(0, n - 1)
            def _(j):
                st_copy(me, peer_of(j)).start()

        returned = jnp.dot(back[...], operm[...], preferred_element_type=jnp.float32)
        retsrc[c] = returned.astype(jnp.bfloat16).reshape(n, part, width)

        @pl.loop(0, n - 1)
        def _(j, c=c):
            ret_copy(c, me, peer_of(j)).start()

        retrecv[c, me] = retsrc[c, me]
        if c == 0:
            own_all().wait_recv()
            eye = iota((req_dev, req_dev), 0) == iota((req_dev, req_dev), 1)
            for s in range(n):
                own_col[s * req_dev:(s + 1) * req_dev] = jnp.sum(
                    jnp.where(eye, own_recv[s].astype(jnp.float32), 0.0), axis=1, keepdims=True
                )
    stats_recv[me] = stats_src[me]

    @pl.loop(1, n // 2)
    def _(j):
        slot = lax.rem(me + 2 * j, n)
        kv_copy(slot, me).wait_recv()
        fw_copy(slot).start()

    @pl.loop(0, n // 2)
    def _(j):
        slot = lax.rem(partner + 2 * j, n)
        fw_copy(slot).wait_recv()

    tokens = n * page_len
    page = div(iota((1, tokens), 1), page_len)
    token_owner = jnp.zeros((1, tokens), jnp.float32)
    end = jnp.int32(0)
    for i in range(pc_ref.shape[0]):
        end = end + pc_ref[i]
        token_owner = token_owner + jnp.where(page >= end, 1.0, 0.0)

    block = max(32, min(rows_all, PREFIX_KI * 1024 // tokens))

    @pl.loop(0, rows_all // block)
    def _(b):
        rows = pl.ds(pl.multiple_of(b * block, block), block)
        live = own_col[rows] == token_owner
        keys = pool[:, :, :head_dim].reshape(tokens, head_dim)
        values = pool[:, :, head_dim:].reshape(tokens, head_dim)
        for h in range(per_dev):
            scores = lax.dot_general(
                q_ref[rows, h * head_dim:(h + 1) * head_dim], keys, (((1,), (1,)), ((), ())),
                preferred_element_type=jnp.float32,
            )
            scores = jnp.where(live, scores, neg_large)
            top_score = jnp.max(scores, axis=1, keepdims=True)
            weight = jnp.exp2((scores - top_score) * scale)
            top[h, rows] = top_score * scale
            total[h, rows] = jnp.sum(weight, axis=1, keepdims=True)
            mix[rows, h * head_dim:(h + 1) * head_dim] = jnp.dot(
                weight.astype(jnp.bfloat16), values, preferred_element_type=jnp.float32
            )

    for c in range(CHUNKS):
        q_all(c).wait_send()
    own_all().wait_send()
    kv_all().wait_send()
    fw_all().wait_send()

    st_all().wait_recv()
    sub, lan = iota((req_dev, LANES), 0), iota((req_dev, LANES), 1)

    @pl.loop(0, n // 2)
    def _(step):
        for u in range(2):
            s = step * 2 + u
            rows = pl.ds(pl.multiple_of(s * req_dev, req_dev), req_dev)
            row = stats_recv[s]
            for h in range(per_dev):
                span = slice(h * head_dim, (h + 1) * head_dim)
                level = jnp.sum(
                    jnp.where(lan == h * req_dev + sub, row, 0.0), axis=1, keepdims=True
                )
                top_first = top[h, rows]
                top_score = jnp.maximum(level, top_first)
                factor_second = jnp.exp2(level - top_score)
                factor_first = jnp.exp2(top_first - top_score)
                inverse = 1.0 / (total[h, rows] * factor_first + factor_second)
                mix[rows, span] = mix[rows, span] * (factor_first * inverse)
                second_factor[rows, span] = jnp.broadcast_to(
                    factor_second * inverse, (req_dev, head_dim)
                )

    def gather_in(c, s):
        rows = pl.ds(pl.multiple_of(s * req_dev + c * part, part), part)
        second = retrecv[c, s].astype(jnp.float32)
        out_ref[rows, :] = (mix[rows, :] + second * second_factor[rows, :]).astype(out_ref.dtype)

    for c in range(CHUNKS):
        gather_in(c, me)

        @pl.loop(0, n - 1)
        def _(j, c=c):
            slot = source_of(j)
            ret_copy(c, slot, me).wait_recv()
            gather_in(c, slot)

    st_all().wait_send()
    for c in range(CHUNKS):
        ret_all(c).wait_send()


def body(queries, prefix_kv, page_counts, request_prefix, suffix_kv, suffix_len):
    n = lax.axis_size("blk")
    rows_all, width = queries.shape
    req_dev, suf_len, kv_heads, kv_width = suffix_kv.shape
    head_dim = kv_width // 2
    per_dev = width // head_dim
    page_len = prefix_kv.shape[1]
    part = req_dev // CHUNKS
    page = prefix_kv.reshape(page_len * kv_heads, kv_width)
    cache = suffix_kv.reshape(req_dev, suf_len * kv_heads, kv_width)
    bf16, f32, i32 = jnp.bfloat16, jnp.float32, jnp.int32
    dma = pltpu.SemaphoreType.DMA
    vmem = pl.BlockSpec(memory_space=pltpu.VMEM)
    smem = pl.BlockSpec(memory_space=pltpu.SMEM)
    anywhere = pl.BlockSpec(memory_space=pl.ANY)
    return pl.pallas_call(
        functools.partial(kernel, n),
        out_shape=pltpu.VMEM((rows_all, width), bf16),
        in_specs=[anywhere, anywhere, vmem, smem, anywhere, smem],
        out_specs=vmem,
        scratch_shapes=[
            pltpu.VMEM((rows_all, width), bf16),
            pltpu.VMEM((page_len * kv_heads, kv_width), bf16),
            pltpu.VMEM((kv_heads, page_len, kv_width), bf16),
            pltpu.VMEM((part * n, part * n), bf16),
            pltpu.VMEM((part * n, part * n), bf16),
            pltpu.VMEM((CHUNKS, n, part, width), bf16),
            pltpu.VMEM((part * n, width), bf16),
            pltpu.VMEM((part * n, width), bf16),
            pltpu.VMEM((CHUNKS, n, part, width), bf16),
            pltpu.VMEM((CHUNKS, n, part, width), bf16),
            pltpu.VMEM((n, page_len, kv_width), bf16),
            pltpu.VMEM((req_dev, suf_len * kv_heads, kv_width), bf16),
            pltpu.VMEM((n, 1, req_dev), i32),
            pltpu.VMEM((rows_all, 1), f32),
            pltpu.VMEM((n, 1, LANES), f32),
            pltpu.VMEM((n, 1, LANES), f32),
            pltpu.VMEM((rows_all, width), f32),
            pltpu.VMEM((rows_all, width), f32),
            pltpu.VMEM((per_dev, rows_all, 1), f32),
            pltpu.VMEM((per_dev, rows_all, 1), f32),
            dma((CHUNKS,)), dma((CHUNKS,)), dma, dma, dma, dma((n,)), dma,
            dma((CHUNKS,)), dma((CHUNKS, n)), dma, dma, dma((req_dev,)), dma((2,)),
        ],
        compiler_params=pltpu.CompilerParams(
            collective_id=0, has_side_effects=True, vmem_limit_bytes=VMEM_MIB * 1024 * 1024
        ),
    )(queries, page, request_prefix.T, page_counts, cache, suffix_len)


def solution(mesh):
    in_specs = (
        P("groups", "blk"),
        P(("groups", "blk"), None, None, None),
        P("groups"),
        P(("groups", "blk"), None),
        P(("groups", "blk"), None, None, None),
        P(("groups", "blk")),
    )
    out_specs = P("groups", "blk")
    return jax.shard_map(body, mesh=mesh, in_specs=in_specs, out_specs=out_specs, check_vma=False)
```

time: 48.5 us -> 39.6 us (0.82)
  Pallas kernels: 46.5 us -> 38.6 us
  local copies, waits for them, and re-layouts: 1.87 us -> 0.8 us
    pallas_call x1, Pallas kernels: 46.5 us -> 38.6 us  [body(): pl.pallas_call(functools.partial(kernel, n), out_shape=pltpu.VMEM((rows_a...]
    unnamed x1, local copies, waits for them, and re-layouts: 1.87 us -> 0.8 us
where the time goes in v1:
time: 39.6 us; the launch traced here: 39.4 us
  Pallas kernels  38.6 us (97%)
  local copies, waits for them, and re-layouts  0.8 us (2%)
    pallas_call x1, Pallas kernels, body(): pl.pallas_call(functools.partial(kernel, n), out_shape=pltpu.VMEM((rows_a...  38.6 us
    unnamed x1, local copies, waits for them, and re-layouts  0.8 us

profile of v1, /device:TPU:13, one launch (start us, length us, event | category | flops | bytes accessed | tf_op | source)
XLA Modules:
  0.0 39.4 jit_solution(18385568954768854745)
XLA Ops:
  0.0 38.6 %shard_map.64 = bf16[512,512]{1,0:T(8,128)(2,1)S(1)} custom-call(bf16[512,512]{1,0:T(8,128)(2,1)} %q_hbm.1, bf16[512,256]{1,0:T(8,128)(2,1)} %bitcast.4, s32[1,32]{1,0:T(1,128)} %bitcast.5, s32[4]{0:T(128)} %pc_ref.1, bf16[32,512,256]{2,1,0:T(8,128)(2,1)} %bitcast.3, s32[32]{0:T(128)} %len_ref.1), custom_call_target="tpu_custom_call" | custom-call | tf_op jit(solution)/shard_map/pallas_call | solution.py:358
  38.6 0.8 %copy.8 = bf16[512,512]{1,0:T(8,128)(2,1)} copy(bf16[512,512]{1,0:T(8,128)(2,1)S(1)} %shard_map.64) | data formatting | bytes 1048576

commit v2 on v1

--- a/solution.py
+++ b/solution.py
@@ -21,11 +21,16 @@
 
 MESH = pl.DeviceIdType.MESH
 CHUNKS = 2
-UNROLL = 4
+UNROLL = 8
 LANES = 128
 PREFIX_KI = 256
 VMEM_MIB = 56
 LOG2E = math.log2(math.e)
+
+
+def plane_of(n):
+    bits = n.bit_length() - 1
+    return 1 << (bits + 1) // 2 if n & (n - 1) == 0 else 1
 
 
 def kernel(
@@ -33,7 +38,7 @@
     q_ref, kv_ref, home, order, back, qrecv, qperm, operm, retsrc, retrecv, pool, suf, own_recv,
     own_col, stats_src, stats_recv, mix, second_factor, top, total,
     q_send, q_recv_sem, own_send, own_recv_sem, kv_send, kv_recv, fw_send,
-    ret_send, ret_recv, st_send, st_recv, suf_sem, in_sem,
+    ret_send, ret_recv, st_send, st_recv, suf_sem, in_sem, from_below, from_above,
 ):
     me = lax.axis_index("blk")
     partner = me + 1 - 2 * lax.rem(me, 2)
@@ -53,13 +58,27 @@
     def iota(shape, dim):
         return lax.broadcasted_iota(jnp.int32, shape, dim)
 
+    def signal(sem, peer):
+        pl.semaphore_signal(sem, inc=1, device_id={"blk": peer}, device_id_type=MESH)
+
     barrier = pltpu.get_barrier_semaphore()
-
-    @pl.loop(1, n)
+    side = plane_of(n)
+    planes = n // side
+    plane, spot = div(me, side), mod(me, side)
+    has_up, has_down = plane + 1 < planes, plane > 0
+    up, down = lax.rem(me + side, n), lax.rem(me + n - side, n)
+
+    @pl.when(has_up)
+    def _():
+        signal(barrier, up)
+
+    @pl.when(has_down)
+    def _():
+        signal(barrier, down)
+
+    @pl.loop(1, side)
     def _(k):
-        pl.semaphore_signal(
-            barrier, inc=1, device_id={"blk": lax.rem(me + k, n)}, device_id_type=MESH
-        )
+        signal(barrier, plane * side + jnp.bitwise_xor(spot, k))
 
     q_in = pltpu.make_async_copy(q_hbm, q_ref, in_sem.at[0])
     kv_in = pltpu.make_async_copy(kv_hbm, kv_ref, in_sem.at[1])
@@ -133,20 +152,61 @@
         some = stats_recv.at[pl.ds(0, n - 1)]
         return send(some, some, st_send, st_recv, partner)
 
+    def q_plane(p, first, last):
+        for c in range(CHUNKS):
+
+            @pl.loop(first, last)
+            def _(i, c=c):
+                q_copy(c, me, p * side + jnp.bitwise_xor(spot, i)).start()
+
     q_in.wait()
-    pl.semaphore_wait(barrier, n - 1)
-
-    for c in range(CHUNKS):
-
-        @pl.loop(0, n - 1)
-        def _(j, c=c):
-            q_copy(c, me, peer_of(j)).start()
-
-        if c == 0:
-
-            @pl.loop(0, n - 1)
-            def _(j):
-                own_copy(me, peer_of(j)).start()
+    neighbours = has_up.astype(jnp.int32) + has_down.astype(jnp.int32)
+    pl.semaphore_wait(barrier, side - 1 + neighbours)
+
+    @pl.when(has_up)
+    def _():
+        signal(from_below.at[1], up)
+        q_plane(plane + 1, 0, 1)
+
+    @pl.when(has_down)
+    def _():
+        signal(from_above.at[1], down)
+        q_plane(plane - 1, 0, 1)
+
+    q_plane(plane, 1, side)
+
+    @pl.loop(1, planes)
+    def _(t):
+        above, below = plane + t < planes, plane >= t
+        first = jnp.where(t == 1, 1, 0)
+
+        @pl.when(above)
+        def _():
+            pl.semaphore_wait(from_above.at[t], 1)
+
+            @pl.when(has_down)
+            def _():
+                signal(from_above.at[t + 1], down)
+
+        @pl.when(below)
+        def _():
+            pl.semaphore_wait(from_below.at[t], 1)
+
+            @pl.when(has_up)
+            def _():
+                signal(from_below.at[t + 1], up)
+
+        @pl.when(above)
+        def _():
+            q_plane(plane + t, first, side)
+
+        @pl.when(below)
+        def _():
+            q_plane(plane - t, first, side)
+
+    @pl.loop(0, n - 1)
+    def _(j):
+        own_copy(me, peer_of(j)).start()
 
     for c in range(CHUNKS):
         qrecv[c, me] = q_ref[pl.ds(pl.multiple_of(me * req_dev + c * part, part), part)]
@@ -184,6 +244,11 @@
     lane = iota((n, LANES), 1)
 
     seen = jnp.zeros((n, LANES), jnp.float32)
+
+    @pl.loop(0, req_dev)
+    def _(r):
+        suf_copy(r).wait()
+
     for c in range(CHUNKS):
         q_all(c).wait_recv()
         qperm[...] = jnp.dot(
@@ -195,7 +260,6 @@
             all_scores = []
             for local in ids:
                 r = c * part + local
-                suf_copy(r).wait()
                 rows = pl.ds(pl.multiple_of(local * n, n), n)
                 qr = jnp.concatenate(
                     [qperm[rows, h * head_dim:(h + 1) * head_dim] for h in range(per_dev)], axis=0
@@ -351,7 +415,7 @@
     page = prefix_kv.reshape(page_len * kv_heads, kv_width)
     cache = suffix_kv.reshape(req_dev, suf_len * kv_heads, kv_width)
     bf16, f32, i32 = jnp.bfloat16, jnp.float32, jnp.int32
-    dma = pltpu.SemaphoreType.DMA
+    dma, regular = pltpu.SemaphoreType.DMA, pltpu.SemaphoreType.REGULAR
     vmem = pl.BlockSpec(memory_space=pltpu.VMEM)
     smem = pl.BlockSpec(memory_space=pltpu.SMEM)
     anywhere = pl.BlockSpec(memory_space=pl.ANY)
@@ -383,6 +447,7 @@
             pltpu.VMEM((per_dev, rows_all, 1), f32),
             dma((CHUNKS,)), dma((CHUNKS,)), dma, dma, dma, dma((n,)), dma,
             dma((CHUNKS,)), dma((CHUNKS, n)), dma, dma, dma((req_dev,)), dma((2,)),
+            regular((n // plane_of(n) + 1,)), regular((n // plane_of(n) + 1,)),
         ],
         compiler_params=pltpu.CompilerParams(
             collective_id=0, has_side_effects=True, vmem_limit_bytes=VMEM_MIB * 1024 * 1024

time: 39.6 us -> 38 us (0.960)
  the two profiles are of different devices: /device:TPU:13 before, /device:TPU:0 now
where the time goes in v2:
time: 38 us; the launch traced here: 37.8 us
  Pallas kernels  37 us (97%)
  local copies, waits for them, and re-layouts  0.8 us (2%)
    pallas_call x1, Pallas kernels, body(): pl.pallas_call(functools.partial(kernel, n), out_shape=pltpu.VMEM((rows_a...  37 us
    unnamed x1, local copies, waits for them, and re-layouts  0.8 us

profile of v2, /device:TPU:0, one launch (start us, length us, event | category | flops | bytes accessed | tf_op | source)
XLA Modules:
  0.0 37.8 jit_solution(17887403888407910507)
XLA Ops:
  0.0 37.0 %shard_map.64 = bf16[512,512]{1,0:T(8,128)(2,1)S(1)} custom-call(bf16[512,512]{1,0:T(8,128)(2,1)} %q_hbm.1, bf16[512,256]{1,0:T(8,128)(2,1)} %bitcast.4, s32[1,32]{1,0:T(1,128)} %bitcast.5, s32[4]{0:T(128)} %pc_ref.1, bf16[32,512,256]{2,1,0:T(8,128)(2,1)} %bitcast.3, s32[32]{0:T(128)} %len_ref.1), custom_call_target="tpu_custom_call" | custom-call | tf_op jit(solution)/shard_map/pallas_call | solution.py:422
  37.1 0.8 %copy.8 = bf16[512,512]{1,0:T(8,128)(2,1)} copy(bf16[512,512]{1,0:T(8,128)(2,1)S(1)} %shard_map.64) | data formatting | bytes 1048576

commit v3 on v1

v3 whole, which is shorter than its diff:
```python
import functools
import math

import jax
import jax.numpy as jnp
from jax import lax
from jax.experimental import pallas as pl
from jax.experimental.pallas import tpu as pltpu
from jax.sharding import PartitionSpec as P

neg_large = -1e30


def div(x, k):
    return jnp.right_shift(x, k.bit_length() - 1) if k & (k - 1) == 0 else x // k


def mod(x, k):
    return jnp.bitwise_and(x, k - 1) if k & (k - 1) == 0 else lax.rem(x, k)


MESH = pl.DeviceIdType.MESH
CHUNKS = 2
UNROLL = 8
LANES = 128
PREFIX_KI = 256
VMEM_MIB = 56
LOG2E = math.log2(math.e)


def plane_of(n):
    bits = n.bit_length() - 1
    return 1 << (bits + 1) // 2 if n & (n - 1) == 0 else 1


def kernel(
    n, q_hbm, kv_hbm, rp_hbm, pc_hbm, suf_ref, len_hbm, out_ref,
    rp_ref, pc_ref, len_ref, q_ref, kv_ref, home, order, back, qrecv, qperm, operm, retsrc, retrecv, pool, suf, own_recv,
    own_col, stats_src, stats_recv, mix, second_factor, top, total,
    q_send, q_recv_sem, own_send, own_recv_sem, kv_send, kv_recv, fw_send,
    ret_send, ret_recv, st_send, st_recv, suf_sem, in_sem, from_below, from_above,
):
    me = lax.axis_index("blk")
    partner = me + 1 - 2 * lax.rem(me, 2)
    rows_all, width = q_ref.shape
    req_dev = rows_all // n
    part = req_dev // CHUNKS
    kv_heads, page_len, kv_width = home.shape
    head_dim = kv_width // 2
    per_dev = width // head_dim
    heads = per_dev * n
    group_size = heads // kv_heads
    share = n // kv_heads
    cols = suf_ref.shape[1]
    scale = head_dim ** -0.5 * LOG2E
    power = n & (n - 1) == 0

    def iota(shape, dim):
        return lax.broadcasted_iota(jnp.int32, shape, dim)

    def signal(sem, peer):
        pl.semaphore_signal(sem, inc=1, device_id={"blk": peer}, device_id_type=MESH)

    barrier = pltpu.get_barrier_semaphore()
    side = plane_of(n)
    planes = n // side
    plane, spot = div(me, side), mod(me, side)
    has_up, has_down = plane + 1 < planes, plane > 0
    up, down = lax.rem(me + side, n), lax.rem(me + n - side, n)

    @pl.loop(0, side)
    def _(k):
        spot_k = jnp.bitwise_xor(spot, k)

        @pl.when(has_up)
        def _():
            signal(barrier, (plane + 1) * side + spot_k)

        @pl.when(has_down)
        def _():
            signal(barrier, (plane - 1) * side + spot_k)

        @pl.when(k > 0)
        def _():
            signal(barrier, plane * side + spot_k)

    q_in = pltpu.make_async_copy(q_hbm, q_ref, in_sem.at[0])
    kv_in = pltpu.make_async_copy(kv_hbm, kv_ref, in_sem.at[1])
    small_in = [
        pltpu.make_async_copy(src, dst, in_sem.at[2 + i])
        for i, (src, dst) in enumerate(((rp_hbm, rp_ref), (pc_hbm, pc_ref), (len_hbm, len_ref)))
    ]
    q_in.start()
    kv_in.start()
    for copy in small_in:
        copy.start()

    def suf_copy(r):
        return pltpu.make_async_copy(suf_ref.at[r], suf.at[r], suf_sem.at[r])

    @pl.loop(0, req_dev)
    def _(r):
        suf_copy(r).start()

    def send(src, dst, s_sem, r_sem, peer):
        return pltpu.make_async_remote_copy(
            src_ref=src, dst_ref=dst, send_sem=s_sem, recv_sem=r_sem,
            device_id={"blk": peer}, device_id_type=MESH,
        )

    half = n // 2 if planes % 2 == 0 else n
    base = div(me, half) * half
    lower = me < half

    def peer_of(j):
        return jnp.bitwise_xor(me, j + 1) if power else lax.rem(me + j + 1, n)

    def local_of(j):
        return jnp.bitwise_xor(me, j + 1) if power else base + lax.rem(me - base + j + 1, half)

    def across_of(t, i):
        p = jnp.where(lower, planes - 1 - t, t)
        return p * side + jnp.bitwise_xor(spot, i)

    def q_copy(c, slot, peer):
        rows = pl.ds(pl.multiple_of(peer * req_dev + c * part, part), part)
        return send(q_ref.at[rows], qrecv.at[c, slot], q_send.at[c], q_recv_sem.at[c], peer)

    def q_all(c):
        some = qrecv.at[c, pl.ds(0, n - 1)]
        return send(some, some, q_send.at[c], q_recv_sem.at[c], partner)

    def own_copy(slot, peer):
        return send(rp_ref, own_recv.at[slot], own_send, own_recv_sem, peer)

    def own_all():
        some = own_recv.at[pl.ds(0, n - 1)]
        return send(some, some, own_send, own_recv_sem, partner)

    def kv_copy(slot, peer):
        return send(home.at[peer // share], pool.at[slot], kv_send, kv_recv.at[slot], peer)

    def kv_all():
        some = pool.at[pl.ds(0, n // 2 - 1)]
        return send(some, some, kv_send, kv_recv.at[0], partner)

    def fw_copy(slot):
        return send(pool.at[slot], pool.at[slot], fw_send, kv_recv.at[slot], partner)

    def fw_own():
        return send(home.at[me // share], pool.at[me], fw_send, kv_recv.at[me], partner)

    def fw_all():
        some = pool.at[pl.ds(0, n // 2)]
        return send(some, some, fw_send, kv_recv.at[0], partner)

    def ret_copy(c, slot, peer):
        return send(
            retsrc.at[c, peer], retrecv.at[c, slot], ret_send.at[c], ret_recv.at[c, slot], peer
        )

    def ret_across(c, first, last):
        @pl.loop(first * side, last * side)
        def _(j):
            ret_copy(c, me, across_of(div(j, side), mod(j, side))).start()

    def ret_all(c):
        some = retsrc.at[c, pl.ds(0, n - 1)]
        return send(some, some, ret_send.at[c], ret_recv.at[c, 0], partner)

    def st_copy(slot, peer):
        return send(stats_src.at[peer], stats_recv.at[slot], st_send, st_recv, peer)

    def st_all():
        some = stats_recv.at[pl.ds(0, n - 1)]
        return send(some, some, st_send, st_recv, partner)

    def q_plane(p, first, last, chunks):
        for c in chunks:

            @pl.loop(first, last)
            def _(i, c=c):
                q_copy(c, me, p * side + jnp.bitwise_xor(spot, i)).start()

    neighbours = has_up.astype(jnp.int32) + has_down.astype(jnp.int32)
    pl.semaphore_wait(barrier, side - 1 + side * neighbours)

    @pl.when(has_up & has_down)
    def _():
        signal(from_below.at[2], up)
        signal(from_above.at[2], down)

    q_in.wait()

    def near(chunks):
        @pl.when(has_up)
        def _():
            q_plane(plane + 1, 0, side, chunks)

        @pl.when(has_down)
        def _():
            q_plane(plane - 1, 0, side, chunks)

        q_plane(plane, 1, side, chunks)

    def far(c, relay):
        @pl.loop(2, planes)
        def _(t):
            above, below = plane + t < planes, plane >= t
            if relay:

                @pl.when(above)
                def _():
                    pl.semaphore_wait(from_above.at[t], 1)

                    @pl.when(has_down)
                    def _():
                        signal(from_above.at[t + 1], down)

                @pl.when(below)
                def _():
                    pl.semaphore_wait(from_below.at[t], 1)

                    @pl.when(has_up)
                    def _():
                        signal(from_below.at[t + 1], up)

            @pl.when(above)
            def _():
                q_plane(plane + t, 0, side, (c,))

            @pl.when(below)
            def _():
                q_plane(plane - t, 0, side, (c,))

    def send_own():
        for copy in small_in:
            copy.wait()

        @pl.loop(0, n - 1)
        def _(j):
            own_copy(me, peer_of(j)).start()

        own_recv[me] = rp_ref[...]

    def keep_mine():
        for c in range(CHUNKS):
            qrecv[c, me] = q_ref[pl.ds(pl.multiple_of(me * req_dev + c * part, part), part)]

    def turn_page():
        kv_in.wait()
        entries = kv_heads * page_len
        entry, source = iota((entries, entries), 0), iota((entries, entries), 1)
        turn = jnp.where(
            source == mod(entry, page_len) * kv_heads + div(entry, page_len), 1.0, 0.0
        ).astype(jnp.bfloat16)
        turned = jnp.dot(turn, kv_ref[...], preferred_element_type=jnp.float32)
        home[...] = turned.astype(jnp.bfloat16).reshape(home.shape)
        pool[me] = home[me // share]

    def send_pages():
        @pl.loop(1, n // 2)
        def _(j):
            kv_copy(me, lax.rem(me + 2 * j, n)).start()

        fw_own().start()

    size = part * n

    def make_orders():
        row_id, col_id = iota((size, size), 0), iota((size, size), 1)
        order[...] = jnp.where(
            col_id == mod(row_id, n) * part + div(row_id, n), 1.0, 0.0
        ).astype(jnp.bfloat16)
        back[...] = jnp.where(
            col_id == mod(row_id, part) * n + div(row_id, part), 1.0, 0.0
        ).astype(jnp.bfloat16)

    def suffix_in():
        @pl.loop(0, req_dev)
        def _(r):
            suf_copy(r).wait()

    def suffix(c, seen):
        stacked = iota((per_dev * n, cols), 0)
        head_of_row = mod(stacked, n) * per_dev + div(stacked, n)
        column = iota((per_dev * n, cols), 1)
        own_kv = div(head_of_row, group_size) == mod(column, kv_heads)
        position = jnp.where(own_kv, div(column, kv_heads), cols)
        lane = iota((n, LANES), 1)
        qperm[...] = jnp.dot(
            order[...], qrecv[c].reshape(size, width), preferred_element_type=jnp.float32
        ).astype(jnp.bfloat16)

        def some_requests(step, seen):
            ids = [step * UNROLL + u for u in range(UNROLL)]
            all_scores = []
            for local in ids:
                rows = pl.ds(pl.multiple_of(local * n, n), n)
                qr = jnp.concatenate(
                    [qperm[rows, h * head_dim:(h + 1) * head_dim] for h in range(per_dev)], axis=0
                )
                all_scores.append(lax.dot_general(
                    qr, suf[c * part + local, :, :head_dim], (((1,), (1,)), ((), ())),
                    preferred_element_type=jnp.float32,
                ))
            for local, scores in zip(ids, all_scores):
                r = c * part + local
                rows = pl.ds(pl.multiple_of(local * n, n), n)
                scores = jnp.where(position < len_ref[r], scores, neg_large)
                top_score = jnp.max(scores, axis=1, keepdims=True)
                weight = jnp.exp2((scores - top_score) * scale)
                weight_sum = jnp.sum(weight, axis=1, keepdims=True)
                mixed = jnp.dot(
                    weight.astype(jnp.bfloat16), suf[r, :, head_dim:],
                    preferred_element_type=jnp.float32,
                )
                result = (mixed * (1.0 / weight_sum)).astype(jnp.bfloat16)
                level = top_score * scale + jnp.log(weight_sum) * LOG2E
                for h in range(per_dev):
                    operm[rows, h * head_dim:(h + 1) * head_dim] = result[h * n:(h + 1) * n]
                    seen = jnp.where(
                        lane == h * req_dev + r, level[h * n:(h + 1) * n], seen
                    )
            return seen

        seen = lax.fori_loop(0, part // UNROLL, some_requests, seen)
        returned = jnp.dot(back[...], operm[...], preferred_element_type=jnp.float32)
        retsrc[c] = returned.astype(jnp.bfloat16).reshape(n, part, width)
        retrecv[c, me] = retsrc[c, me]
        return seen

    def send_stats(seen):
        for p in range(n):
            stats_src[p] = seen[p:p + 1, :]

        @pl.loop(0, n - 1)
        def _(j):
            st_copy(me, peer_of(j)).start()

        stats_recv[me] = stats_src[me]

    def send_back_near(c):
        @pl.loop(0, half - 1)
        def _(j):
            ret_copy(c, me, local_of(j)).start()

    def send_back_across(c):
        if half < n:
            ret_across(c, 0, planes // 2)

    def take_own():
        own_all().wait_recv()
        eye = iota((req_dev, req_dev), 0) == iota((req_dev, req_dev), 1)
        for s in range(n):
            own_col[s * req_dev:(s + 1) * req_dev] = jnp.sum(
                jnp.where(eye, own_recv[s].astype(jnp.float32), 0.0), axis=1, keepdims=True
            )

    def pass_pages():
        @pl.loop(1, n // 2)
        def _(j):
            slot = lax.rem(me + 2 * j, n)
            kv_copy(slot, me).wait_recv()
            fw_copy(slot).start()

    def take_pages():
        @pl.loop(0, n // 2)
        def _(j):
            slot = lax.rem(partner + 2 * j, n)
            fw_copy(slot).wait_recv()

    def prefix():
        tokens = n * page_len
        page = div(iota((1, tokens), 1), page_len)
        token_owner = jnp.zeros((1, tokens), jnp.float32)
        end = jnp.int32(0)
        for i in range(pc_ref.shape[0]):
            end = end + pc_ref[i]
            token_owner = token_owner + jnp.where(page >= end, 1.0, 0.0)

        block = max(32, min(rows_all, PREFIX_KI * 1024 // tokens))

        @pl.loop(0, rows_all // block)
        def _(b):
            rows = pl.ds(pl.multiple_of(b * block, block), block)
            live = own_col[rows] == token_owner
            keys = pool[:, :, :head_dim].reshape(tokens, head_dim)
            values = pool[:, :, head_dim:].reshape(tokens, head_dim)
            for h in range(per_dev):
                span = slice(h * head_dim, (h + 1) * head_dim)
                scores = lax.dot_general(
                    q_ref[rows, span], keys, (((1,), (1,)), ((), ())),
                    preferred_element_type=jnp.float32,
                )
                scores = jnp.where(live, scores, neg_large)
                top_score = jnp.max(scores, axis=1, keepdims=True)
                weight = jnp.exp2((scores - top_score) * scale)
                top[h, rows] = top_score * scale
                total[h, rows] = jnp.sum(weight, axis=1, keepdims=True)
                mix[rows, span] = jnp.dot(
                    weight.astype(jnp.bfloat16), values, preferred_element_type=jnp.float32
                )

    def factors():
        st_all().wait_recv()
        sub, lan = iota((req_dev, LANES), 0), iota((req_dev, LANES), 1)

        @pl.loop(0, n // 2)
        def _(step):
            for u in range(2):
                s = step * 2 + u
                rows = pl.ds(pl.multiple_of(s * req_dev, req_dev), req_dev)
                row = stats_recv[s]
                for h in range(per_dev):
                    span = slice(h * head_dim, (h + 1) * head_dim)
                    level = jnp.sum(
                        jnp.where(lan == h * req_dev + sub, row, 0.0), axis=1, keepdims=True
                    )
                    top_first = top[h, rows]
                    top_score = jnp.maximum(level, top_first)
                    factor_second = jnp.exp2(level - top_score)
                    factor_first = jnp.exp2(top_first - top_score)
                    inverse = 1.0 / (total[h, rows] * factor_first + factor_second)
                    mix[rows, span] = mix[rows, span] * (factor_first * inverse)
                    second_factor[rows, span] = jnp.broadcast_to(
                        factor_second * inverse, (req_dev, head_dim)
                    )

    def gather_in(c, s):
        rows = pl.ds(pl.multiple_of(s * req_dev + c * part, part), part)
        second = retrecv[c, s].astype(jnp.float32)
        out_ref[rows, :] = (mix[rows, :] + second * second_factor[rows, :]).astype(out_ref.dtype)

    def arrive(c, slot):
        ret_copy(c, slot, me).wait_recv()
        gather_in(c, slot)

    def gather_near(c):
        gather_in(c, me)

        @pl.loop(0, half - 1)
        def _(j):
            arrive(c, local_of(j))

    def gather_across(c):
        if half < n:

            @pl.loop(0, half)
            def _(j):
                arrive(c, across_of(div(j, side), mod(j, side)))

    seen = jnp.zeros((n, LANES), jnp.float32)
    near((0, 1))
    far(0, True)
    far(1, False)
    send_own()
    keep_mine()
    turn_page()
    send_pages()
    make_orders()
    suffix_in()
    q_all(0).wait_recv()
    seen = suffix(0, seen)
    send_back_near(0)
    send_back_across(0)
    take_own()
    q_all(1).wait_recv()
    seen = suffix(1, seen)
    send_stats(seen)
    send_back_near(1)
    send_back_across(1)
    pass_pages()
    take_pages()
    prefix()
    q_all(0).wait_send()
    q_all(1).wait_send()
    own_all().wait_send()
    kv_all().wait_send()
    fw_all().wait_send()
    factors()
    gather_near(0)
    gather_near(1)
    gather_across(0)
    gather_across(1)
    st_all().wait_send()
    ret_all(0).wait_send()
    ret_all(1).wait_send()


def body(queries, prefix_kv, page_counts, request_prefix, suffix_kv, suffix_len):
    n = lax.axis_size("blk")
    rows_all, width = queries.shape
    req_dev, suf_len, kv_heads, kv_width = suffix_kv.shape
    head_dim = kv_width // 2
    per_dev = width // head_dim
    page_len = prefix_kv.shape[1]
    part = req_dev // CHUNKS
    page = prefix_kv.reshape(page_len * kv_heads, kv_width)
    cache = suffix_kv.reshape(req_dev, suf_len * kv_heads, kv_width)
    bf16, f32, i32 = jnp.bfloat16, jnp.float32, jnp.int32
    dma, regular = pltpu.SemaphoreType.DMA, pltpu.SemaphoreType.REGULAR
    vmem = pl.BlockSpec(memory_space=pltpu.VMEM)
    anywhere = pl.BlockSpec(memory_space=pl.ANY)
    return pl.pallas_call(
        functools.partial(kernel, n),
        out_shape=pltpu.VMEM((rows_all, width), bf16),
        in_specs=[anywhere] * 6,
        out_specs=vmem,
        scratch_shapes=[
            pltpu.VMEM((1, req_dev), i32),
            pltpu.SMEM(page_counts.shape, i32),
            pltpu.SMEM((req_dev,), i32),
            pltpu.VMEM((rows_all, width), bf16),
            pltpu.VMEM((page_len * kv_heads, kv_width), bf16),
            pltpu.VMEM((kv_heads, page_len, kv_width), bf16),
            pltpu.VMEM((part * n, part * n), bf16),
            pltpu.VMEM((part * n, part * n), bf16),
            pltpu.VMEM((CHUNKS, n, part, width), bf16),
            pltpu.VMEM((part * n, width), bf16),
            pltpu.VMEM((part * n, width), bf16),
            pltpu.VMEM((CHUNKS, n, part, width), bf16),
            pltpu.VMEM((CHUNKS, n, part, width), bf16),
            pltpu.VMEM((n, page_len, kv_width), bf16),
            pltpu.VMEM((req_dev, suf_len * kv_heads, kv_width), bf16),
            pltpu.VMEM((n, 1, req_dev), i32),
            pltpu.VMEM((rows_all, 1), f32),
            pltpu.VMEM((n, 1, LANES), f32),
            pltpu.VMEM((n, 1, LANES), f32),
            pltpu.VMEM((rows_all, width), f32),
            pltpu.VMEM((rows_all, width), f32),
            pltpu.VMEM((per_dev, rows_all, 1), f32),
            pltpu.VMEM((per_dev, rows_all, 1), f32),
            dma((CHUNKS,)), dma((CHUNKS,)), dma, dma, dma, dma((n,)), dma,
            dma((CHUNKS,)), dma((CHUNKS, n)), dma, dma, dma((req_dev,)), dma((5,)),
            regular((n // plane_of(n) + 1,)), regular((n // plane_of(n) + 1,)),
        ],
        compiler_params=pltpu.CompilerParams(
            collective_id=0, has_side_effects=True, vmem_limit_bytes=VMEM_MIB * 1024 * 1024
        ),
    )(queries, page, request_prefix.T, page_counts, cache, suffix_len)


def solution(mesh):
    in_specs = (
        P("groups", "blk"),
        P(("groups", "blk"), None, None, None),
        P("groups"),
        P(("groups", "blk"), None),
        P(("groups", "blk"), None, None, None),
        P(("groups", "blk")),
    )
    out_specs = P("groups", "blk")
    return jax.shard_map(body, mesh=mesh, in_specs=in_specs, out_specs=out_specs, check_vma=False)
```

time: 39.6 us -> 36.4 us (0.919)
  the two profiles are of different devices: /device:TPU:13 before, /device:TPU:0 now
where the time goes in v3:
time: 36.4 us; the launch traced here: 35.9 us
  Pallas kernels  35.1 us (96%)
  local copies, waits for them, and re-layouts  0.8 us (2%)
    pallas_call x1, Pallas kernels, body(): pl.pallas_call(functools.partial(kernel, n), out_shape=pltpu.VMEM((rows_a...  35.1 us
    unnamed x1, local copies, waits for them, and re-layouts  0.8 us

profile of v3, /device:TPU:0, one launch (start us, length us, event | category | flops | bytes accessed | tf_op | source)
XLA Modules:
  0.0 35.9 jit_solution(11470696802850302097)
XLA Ops:
  0.0 35.1 %shard_map.64 = bf16[512,512]{1,0:T(8,128)(2,1)S(1)} custom-call(bf16[512,512]{1,0:T(8,128)(2,1)} %q_hbm.1, bf16[512,256]{1,0:T(8,128)(2,1)} %bitcast.4, s32[1,32]{1,0:T(1,128)} %bitcast.5, s32[4]{0:T(128)} %pc_hbm.1, bf16[32,512,256]{2,1,0:T(8,128)(2,1)} %bitcast.3, s32[32]{0:T(128)} %len_hbm.1), custom_call_target="tpu_custom_call" | custom-call | tf_op jit(solution)/shard_map/pallas_call | solution.py:505
  35.1 0.8 %copy.8 = bf16[512,512]{1,0:T(8,128)(2,1)} copy(bf16[512,512]{1,0:T(8,128)(2,1)S(1)} %shard_map.64) | data formatting | bytes 1048576

commit v4 on v3

--- a/solution.py
+++ b/solution.py
@@ -22,6 +22,7 @@
 MESH = pl.DeviceIdType.MESH
 CHUNKS = 2
 UNROLL = 8
+NEAR = 1
 LANES = 128
 PREFIX_KI = 256
 VMEM_MIB = 56
@@ -37,8 +38,8 @@
     n, q_hbm, kv_hbm, rp_hbm, pc_hbm, suf_ref, len_hbm, out_ref,
     rp_ref, pc_ref, len_ref, q_ref, kv_ref, home, order, back, qrecv, qperm, operm, retsrc, retrecv, pool, suf, own_recv,
     own_col, stats_src, stats_recv, mix, second_factor, top, total,
-    q_send, q_recv_sem, own_send, own_recv_sem, kv_send, kv_recv, fw_send,
-    ret_send, ret_recv, st_send, st_recv, suf_sem, in_sem, from_below, from_above,
+    q_send, q_recv_sem, own_send, own_recv_sem, kv_send, kv_recv, fw_send, fw_recv,
+    ret_send, ret_recv, st_send, st_recv, suf_sem, in_sem, reply,
 ):
     me = lax.axis_index("blk")
     partner = me + 1 - 2 * lax.rem(me, 2)
@@ -65,24 +66,10 @@
     side = plane_of(n)
     planes = n // side
     plane, spot = div(me, side), mod(me, side)
-    has_up, has_down = plane + 1 < planes, plane > 0
-    up, down = lax.rem(me + side, n), lax.rem(me + n - side, n)
-
-    @pl.loop(0, side)
-    def _(k):
-        spot_k = jnp.bitwise_xor(spot, k)
-
-        @pl.when(has_up)
-        def _():
-            signal(barrier, (plane + 1) * side + spot_k)
-
-        @pl.when(has_down)
-        def _():
-            signal(barrier, (plane - 1) * side + spot_k)
-
-        @pl.when(k > 0)
-        def _():
-            signal(barrier, plane * side + spot_k)
+
+    @pl.loop(me + 1, n)
+    def _(p):
+        signal(barrier, p)
 
     q_in = pltpu.make_async_copy(q_hbm, q_ref, in_sem.at[0])
     kv_in = pltpu.make_async_copy(kv_hbm, kv_ref, in_sem.at[1])
@@ -96,7 +83,7 @@
         copy.start()
 
     def suf_copy(r):
-        return pltpu.make_async_copy(suf_ref.at[r], suf.at[r], suf_sem.at[r])
+        return pltpu.make_async_copy(suf_ref.at[r], suf.at[r], suf_sem)
 
     @pl.loop(0, req_dev)
     def _(r):
@@ -111,6 +98,7 @@
     half = n // 2 if planes % 2 == 0 else n
     base = div(me, half) * half
     lower = me < half
+    middle = (plane == planes // 2) | (plane == planes // 2 - 1)
 
     def peer_of(j):
         return jnp.bitwise_xor(me, j + 1) if power else lax.rem(me + j + 1, n)
@@ -138,31 +126,31 @@
         return send(some, some, own_send, own_recv_sem, partner)
 
     def kv_copy(slot, peer):
-        return send(home.at[peer // share], pool.at[slot], kv_send, kv_recv.at[slot], peer)
+        return send(home.at[peer // share], pool.at[slot], kv_send, kv_recv, peer)
 
     def kv_all():
         some = pool.at[pl.ds(0, n // 2 - 1)]
-        return send(some, some, kv_send, kv_recv.at[0], partner)
+        return send(some, some, kv_send, kv_recv, partner)
 
     def fw_copy(slot):
-        return send(pool.at[slot], pool.at[slot], fw_send, kv_recv.at[slot], partner)
+        return send(pool.at[slot], pool.at[slot], fw_send, fw_recv, partner)
 
     def fw_own():
-        return send(home.at[me // share], pool.at[me], fw_send, kv_recv.at[me], partner)
+        return send(home.at[me // share], pool.at[me], fw_send, fw_recv, partner)
 
     def fw_all():
         some = pool.at[pl.ds(0, n // 2)]
-        return send(some, some, fw_send, kv_recv.at[0], partner)
-
-    def ret_copy(c, slot, peer):
+        return send(some, some, fw_send, fw_recv, partner)
+
+    def ret_copy(c, slot, peer, group):
         return send(
-            retsrc.at[c, peer], retrecv.at[c, slot], ret_send.at[c], ret_recv.at[c, slot], peer
+            retsrc.at[c, peer], retrecv.at[c, slot], ret_send.at[c], ret_recv.at[c, group], peer
         )
 
     def ret_across(c, first, last):
         @pl.loop(first * side, last * side)
         def _(j):
-            ret_copy(c, me, across_of(div(j, side), mod(j, side))).start()
+            ret_copy(c, me, across_of(div(j, side), mod(j, side)), 1).start()
 
     def ret_all(c):
         some = retsrc.at[c, pl.ds(0, n - 1)]
@@ -175,63 +163,60 @@
         some = stats_recv.at[pl.ds(0, n - 1)]
         return send(some, some, st_send, st_recv, partner)
 
-    def q_plane(p, first, last, chunks):
-        for c in chunks:
-
-            @pl.loop(first, last)
-            def _(i, c=c):
-                q_copy(c, me, p * side + jnp.bitwise_xor(spot, i)).start()
-
-    neighbours = has_up.astype(jnp.int32) + has_down.astype(jnp.int32)
-    pl.semaphore_wait(barrier, side - 1 + side * neighbours)
-
-    @pl.when(has_up & has_down)
+    @pl.when(me > 0)
     def _():
-        signal(from_below.at[2], up)
-        signal(from_above.at[2], down)
+        pl.semaphore_wait(barrier, me)
+
+
+    @pl.loop(0, me)
+    def _(j):
+        signal(reply.at[me], me - 1 - j)
 
     q_in.wait()
-
-    def near(chunks):
-        @pl.when(has_up)
-        def _():
-            q_plane(plane + 1, 0, side, chunks)
-
-        @pl.when(has_down)
-        def _():
-            q_plane(plane - 1, 0, side, chunks)
-
-        q_plane(plane, 1, side, chunks)
-
-    def far(c, relay):
-        @pl.loop(2, planes)
-        def _(t):
-            above, below = plane + t < planes, plane >= t
-            if relay:
-
-                @pl.when(above)
-                def _():
-                    pl.semaphore_wait(from_above.at[t], 1)
-
-                    @pl.when(has_down)
-                    def _():
-                        signal(from_above.at[t + 1], down)
-
-                @pl.when(below)
-                def _():
-                    pl.semaphore_wait(from_below.at[t], 1)
-
-                    @pl.when(has_up)
-                    def _():
-                        signal(from_below.at[t + 1], up)
-
-            @pl.when(above)
+    def home_plane(c, later):
+        @pl.loop(1, side)
+        def _(i):
+            p = plane * side + jnp.bitwise_xor(spot, i)
+
+            @pl.when(p > me if later else p < me)
             def _():
-                q_plane(plane + t, 0, side, (c,))
-
-            @pl.when(below)
-            def _():
-                q_plane(plane - t, 0, side, (c,))
+                if later and c == 0:
+                    pl.semaphore_wait(reply.at[p], 1)
+                q_copy(c, me, p).start()
+
+    def to_plane(c, z, wait):
+        @pl.loop(0, side)
+        def _(i):
+            p = z * side + jnp.bitwise_xor(spot, i)
+            if wait:
+                pl.semaphore_wait(reply.at[p], 1)
+            q_copy(c, me, p).start()
+
+    def to_earlier(c):
+        home_plane(c, False)
+
+        @pl.loop(0, plane)
+        def _(j):
+            to_plane(c, plane - 1 - j, False)
+
+    def to_later():
+        home_plane(0, True)
+        home_plane(1, True)
+        reach = jnp.minimum(plane + NEAR, planes)
+
+        @pl.loop(plane + 1, reach)
+        def _(z):
+            to_plane(0, z, True)
+            to_plane(1, z, False)
+
+        @pl.loop(reach, planes)
+        def _(z):
+            to_plane(0, z, True)
+
+    def to_last():
+        @pl.loop(jnp.minimum(plane + NEAR, planes), planes)
+        def _(z):
+            to_plane(1, z, False)
 
     def send_own():
         for copy in small_in:
@@ -277,9 +262,7 @@
         ).astype(jnp.bfloat16)
 
     def suffix_in():
-        @pl.loop(0, req_dev)
-        def _(r):
-            suf_copy(r).wait()
+        pltpu.make_async_copy(suf_ref, suf, suf_sem).wait()
 
     def suffix(c, seen):
         stacked = iota((per_dev * n, cols), 0)
@@ -343,11 +326,22 @@
     def send_back_near(c):
         @pl.loop(0, half - 1)
         def _(j):
-            ret_copy(c, me, local_of(j)).start()
-
-    def send_back_across(c):
+            ret_copy(c, me, local_of(j), 0).start()
+
+    def send_back_across(c, part=0):
         if half < n:
-            ret_across(c, 0, planes // 2)
+            if part == 0:
+                ret_across(c, 0, planes // 2 - 1)
+
+                @pl.when(jnp.logical_not(middle))
+                def _():
+                    ret_across(c, planes // 2 - 1, planes // 2)
+
+            else:
+
+                @pl.when(middle)
+                def _():
+                    ret_across(c, planes // 2 - 1, planes // 2)
 
     def take_own():
         own_all().wait_recv()
@@ -358,17 +352,15 @@
             )
 
     def pass_pages():
+        kv_all().wait_recv()
+
         @pl.loop(1, n // 2)
         def _(j):
             slot = lax.rem(me + 2 * j, n)
-            kv_copy(slot, me).wait_recv()
             fw_copy(slot).start()
 
     def take_pages():
-        @pl.loop(0, n // 2)
-        def _(j):
-            slot = lax.rem(partner + 2 * j, n)
-            fw_copy(slot).wait_recv()
+        fw_all().wait_recv()
 
     def prefix():
         tokens = n * page_len
@@ -432,44 +424,48 @@
         second = retrecv[c, s].astype(jnp.float32)
         out_ref[rows, :] = (mix[rows, :] + second * second_factor[rows, :]).astype(out_ref.dtype)
 
-    def arrive(c, slot):
-        ret_copy(c, slot, me).wait_recv()
-        gather_in(c, slot)
+    def arrived(c, count, group):
+        some = retrecv.at[c, pl.ds(0, count)]
+        send(some, some, ret_send.at[c], ret_recv.at[c, group], partner).wait_recv()
 
     def gather_near(c):
         gather_in(c, me)
+        arrived(c, half - 1, 0)
 
         @pl.loop(0, half - 1)
         def _(j):
-            arrive(c, local_of(j))
+            gather_in(c, local_of(j))
 
     def gather_across(c):
         if half < n:
+            arrived(c, half, 1)
 
             @pl.loop(0, half)
             def _(j):
-                arrive(c, across_of(div(j, side), mod(j, side)))
+                gather_in(c, across_of(div(j, side), mod(j, side)))
 
     seen = jnp.zeros((n, LANES), jnp.float32)
-    near((0, 1))
-    far(0, True)
-    far(1, False)
+    to_earlier(0)
+    to_later()
     send_own()
     keep_mine()
     turn_page()
+    make_orders()
+    to_earlier(1)
+    to_last()
     send_pages()
-    make_orders()
     suffix_in()
     q_all(0).wait_recv()
     seen = suffix(0, seen)
     send_back_near(0)
-    send_back_across(0)
-    take_own()
+    send_back_across(0); send_back_across(0, 1)
     q_all(1).wait_recv()
     seen = suffix(1, seen)
     send_stats(seen)
     send_back_near(1)
     send_back_across(1)
+    send_back_across(1, 1)
+    take_own()
     pass_pages()
     take_pages()
     prefix()
@@ -531,9 +527,9 @@
             pltpu.VMEM((rows_all, width), f32),
             pltpu.VMEM((per_dev, rows_all, 1), f32),
             pltpu.VMEM((per_dev, rows_all, 1), f32),
-            dma((CHUNKS,)), dma((CHUNKS,)), dma, dma, dma, dma((n,)), dma,
-            dma((CHUNKS,)), dma((CHUNKS, n)), dma, dma, dma((req_dev,)), dma((5,)),
-            regular((n // plane_of(n) + 1,)), regular((n // plane_of(n) + 1,)),
+            dma((CHUNKS,)), dma((CHUNKS,)), dma, dma, dma, dma, dma, dma,
+            dma((CHUNKS,)), dma((CHUNKS, 2)), dma, dma, dma, dma((5,)),
+            regular((n,)),
         ],
         compiler_params=pltpu.CompilerParams(
             collective_id=0, has_side_effects=True, vmem_limit_bytes=VMEM_MIB * 1024 * 1024

time: 36.4 us -> 35 us (0.962); the launches traced: 35.9 us -> 34.9 us
  Pallas kernels: 35.1 us -> 34.1 us
    pallas_call x1, Pallas kernels: 35.1 us -> 34.1 us  [body(): pl.pallas_call(functools.partial(kernel, n), out_shape=pltpu.VMEM((rows_a...]
where the time goes in v4:
time: 35 us; the launch traced here: 34.9 us
  Pallas kernels  34.1 us (97%)
  local copies, waits for them, and re-layouts  0.8 us (2%)
    pallas_call x1, Pallas kernels, body(): pl.pallas_call(functools.partial(kernel, n), out_shape=pltpu.VMEM((rows_a...  34.1 us
    unnamed x1, local copies, waits for them, and re-layouts  0.8 us

profile of v4, /device:TPU:0, one launch (start us, length us, event | category | flops | bytes accessed | tf_op | source)
XLA Modules:
  0.0 34.9 jit_solution(12938488939847888469)
XLA Ops:
  0.0 34.1 %shard_map.64 = bf16[512,512]{1,0:T(8,128)(2,1)S(1)} custom-call(bf16[512,512]{1,0:T(8,128)(2,1)} %q_hbm.1, bf16[512,256]{1,0:T(8,128)(2,1)} %bitcast.4, s32[1,32]{1,0:T(1,128)} %bitcast.5, s32[4]{0:T(128)} %pc_hbm.1, bf16[32,512,256]{2,1,0:T(8,128)(2,1)} %bitcast.3, s32[32]{0:T(128)} %len_hbm.1), custom_call_target="tpu_custom_call" | custom-call | tf_op jit(solution)/shard_map/pallas_call | solution.py:501
  34.1 0.8 %copy.8 = bf16[512,512]{1,0:T(8,128)(2,1)} copy(bf16[512,512]{1,0:T(8,128)(2,1)S(1)} %shard_map.64) | data formatting | bytes 1048576

commit v5 on v4

--- a/solution.py
+++ b/solution.py
@@ -37,7 +37,7 @@
 def kernel(
     n, q_hbm, kv_hbm, rp_hbm, pc_hbm, suf_ref, len_hbm, out_ref,
     rp_ref, pc_ref, len_ref, q_ref, kv_ref, home, order, back, qrecv, qperm, operm, retsrc, retrecv, pool, suf, own_recv,
-    own_col, stats_src, stats_recv, mix, second_factor, top, total,
+    own_col, stats_src, stats_recv, mix, second_factor, first_level,
     q_send, q_recv_sem, own_send, own_recv_sem, kv_send, kv_recv, fw_send, fw_recv,
     ret_send, ret_recv, st_send, st_recv, suf_sem, in_sem, reply,
 ):
@@ -388,11 +388,11 @@
                 scores = jnp.where(live, scores, neg_large)
                 top_score = jnp.max(scores, axis=1, keepdims=True)
                 weight = jnp.exp2((scores - top_score) * scale)
-                top[h, rows] = top_score * scale
-                total[h, rows] = jnp.sum(weight, axis=1, keepdims=True)
+                weight_sum = jnp.sum(weight, axis=1, keepdims=True)
+                first_level[h, rows] = top_score * scale + jnp.log(weight_sum) * LOG2E
                 mix[rows, span] = jnp.dot(
                     weight.astype(jnp.bfloat16), values, preferred_element_type=jnp.float32
-                )
+                ) * (1.0 / weight_sum)
 
     def factors():
         st_all().wait_recv()
@@ -409,20 +409,17 @@
                     level = jnp.sum(
                         jnp.where(lan == h * req_dev + sub, row, 0.0), axis=1, keepdims=True
                     )
-                    top_first = top[h, rows]
-                    top_score = jnp.maximum(level, top_first)
-                    factor_second = jnp.exp2(level - top_score)
-                    factor_first = jnp.exp2(top_first - top_score)
-                    inverse = 1.0 / (total[h, rows] * factor_first + factor_second)
-                    mix[rows, span] = mix[rows, span] * (factor_first * inverse)
+                    share_of_second = 1.0 / (1.0 + jnp.exp2(first_level[h, rows] - level))
                     second_factor[rows, span] = jnp.broadcast_to(
-                        factor_second * inverse, (req_dev, head_dim)
+                        share_of_second, (req_dev, head_dim)
                     )
 
     def gather_in(c, s):
         rows = pl.ds(pl.multiple_of(s * req_dev + c * part, part), part)
         second = retrecv[c, s].astype(jnp.float32)
-        out_ref[rows, :] = (mix[rows, :] + second * second_factor[rows, :]).astype(out_ref.dtype)
+        first = mix[rows, :]
+        mixed = first + (second - first) * second_factor[rows, :]
+        out_ref[rows, :] = mixed.astype(out_ref.dtype)
 
     def arrived(c, count, group):
         some = retrecv.at[c, pl.ds(0, count)]
@@ -451,6 +448,7 @@
     keep_mine()
     turn_page()
     make_orders()
+    q_all(0).wait_send()
     to_earlier(1)
     to_last()
     send_pages()
@@ -469,10 +467,9 @@
     pass_pages()
     take_pages()
     prefix()
-    q_all(0).wait_send()
     q_all(1).wait_send()
+    kv_all().wait_send()
     own_all().wait_send()
-    kv_all().wait_send()
     fw_all().wait_send()
     factors()
     gather_near(0)
@@ -526,7 +523,6 @@
             pltpu.VMEM((rows_all, width), f32),
             pltpu.VMEM((rows_all, width), f32),
             pltpu.VMEM((per_dev, rows_all, 1), f32),
-            pltpu.VMEM((per_dev, rows_all, 1), f32),
             dma((CHUNKS,)), dma((CHUNKS,)), dma, dma, dma, dma, dma, dma,
             dma((CHUNKS,)), dma((CHUNKS, 2)), dma, dma, dma, dma((5,)),
             regular((n,)),

time: 35 us -> 35 us (level)
  no operation moved by 1% of the time
where the time goes in v5:
time: 35 us; the launch traced here: 34.9 us
  Pallas kernels  34.1 us (97%)
  local copies, waits for them, and re-layouts  0.8 us (2%)
    pallas_call x1, Pallas kernels, body(): pl.pallas_call(functools.partial(kernel, n), out_shape=pltpu.VMEM((rows_a...  34.1 us
    unnamed x1, local copies, waits for them, and re-layouts  0.8 us

profile of v5, /device:TPU:0, one launch (start us, length us, event | category | flops | bytes accessed | tf_op | source)
XLA Modules:
  0.0 34.9 jit_solution(17949768365621807157)
XLA Ops:
  0.0 34.1 %shard_map.64 = bf16[512,512]{1,0:T(8,128)(2,1)S(1)} custom-call(bf16[512,512]{1,0:T(8,128)(2,1)} %q_hbm.1, bf16[512,256]{1,0:T(8,128)(2,1)} %bitcast.4, s32[1,32]{1,0:T(1,128)} %bitcast.5, s32[4]{0:T(128)} %pc_hbm.1, bf16[32,512,256]{2,1,0:T(8,128)(2,1)} %bitcast.3, s32[32]{0:T(128)} %len_hbm.1), custom_call_target="tpu_custom_call" | custom-call | tf_op jit(solution)/shard_map/pallas_call | solution.py:498
  34.1 0.8 %copy.8 = bf16[512,512]{1,0:T(8,128)(2,1)} copy(bf16[512,512]{1,0:T(8,128)(2,1)S(1)} %shard_map.64) | data formatting | bytes 1048576

commit v6 on v5

--- a/solution.py
+++ b/solution.py
@@ -263,6 +263,16 @@
 
     def suffix_in():
         pltpu.make_async_copy(suf_ref, suf, suf_sem).wait()
+
+    def send_stats(seen):
+        for p in range(n):
+            stats_src[p] = seen[p:p + 1, :]
+
+        @pl.loop(0, n - 1)
+        def _(j):
+            st_copy(me, peer_of(j)).start()
+
+        stats_recv[me] = stats_src[me]
 
     def suffix(c, seen):
         stacked = iota((per_dev * n, cols), 0)
@@ -308,20 +318,12 @@
             return seen
 
         seen = lax.fori_loop(0, part // UNROLL, some_requests, seen)
+        if c == CHUNKS - 1:
+            send_stats(seen)
         returned = jnp.dot(back[...], operm[...], preferred_element_type=jnp.float32)
         retsrc[c] = returned.astype(jnp.bfloat16).reshape(n, part, width)
         retrecv[c, me] = retsrc[c, me]
         return seen
-
-    def send_stats(seen):
-        for p in range(n):
-            stats_src[p] = seen[p:p + 1, :]
-
-        @pl.loop(0, n - 1)
-        def _(j):
-            st_copy(me, peer_of(j)).start()
-
-        stats_recv[me] = stats_src[me]
 
     def send_back_near(c):
         @pl.loop(0, half - 1)
@@ -459,7 +461,7 @@
     send_back_across(0); send_back_across(0, 1)
     q_all(1).wait_recv()
     seen = suffix(1, seen)
-    send_stats(seen)
+    pass
     send_back_near(1)
     send_back_across(1)
     send_back_across(1, 1)

time: 35 us -> 35 us (level)
  no operation moved by 1% of the time
where the time goes in v6:
time: 35 us; the launch traced here: 34.9 us
  Pallas kernels  34.1 us (97%)
  local copies, waits for them, and re-layouts  0.8 us (2%)
    pallas_call x1, Pallas kernels, body(): pl.pallas_call(functools.partial(kernel, n), out_shape=pltpu.VMEM((rows_a...  34.1 us
    unnamed x1, local copies, waits for them, and re-layouts  0.8 us

profile of v6, /device:TPU:0, one launch (start us, length us, event | category | flops | bytes accessed | tf_op | source)
XLA Modules:
  0.0 34.9 jit_solution(13502770168464900090)
XLA Ops:
  0.0 34.1 %shard_map.64 = bf16[512,512]{1,0:T(8,128)(2,1)S(1)} custom-call(bf16[512,512]{1,0:T(8,128)(2,1)} %q_hbm.1, bf16[512,256]{1,0:T(8,128)(2,1)} %bitcast.4, s32[1,32]{1,0:T(1,128)} %bitcast.5, s32[4]{0:T(128)} %pc_hbm.1, bf16[32,512,256]{2,1,0:T(8,128)(2,1)} %bitcast.3, s32[32]{0:T(128)} %len_hbm.1), custom_call_target="tpu_custom_call" | custom-call | tf_op jit(solution)/shard_map/pallas_call | solution.py:500
  34.1 0.8 %copy.8 = bf16[512,512]{1,0:T(8,128)(2,1)} copy(bf16[512,512]{1,0:T(8,128)(2,1)S(1)} %shard_map.64) | data formatting | bytes 1048576
